TPU v7x, 32 devices: a whole 2x2x4 slice. The times are simulated.
32 devices in a mesh: fsdp: 8 (over z, core), cols: 4 (over y, x).
Axes of the slice: x: 2, y: 2, z: 4, core: 2. Of those that a mesh axis runs over, the one named last changes fastest.
Arguments:
- one_query: float32 [4096, 4096], P('fsdp', 'cols'), may hold values from -0.125 to 0.125
- other_query: float32 [4096, 4096], P('fsdp', 'cols'), may hold values from -0.09375 to 0.09375
- one_key: float32 [4096, 4096], P('fsdp', 'cols'), may hold values from -0.125 to 0.125
- other_key: float32 [4096, 4096], P('fsdp', 'cols'), may hold values from -0.09375 to 0.09375
- one_value: float32 [4096, 4096], P('fsdp', 'cols'), may hold values from -0.125 to 0.125
- other_value: float32 [4096, 4096], P('fsdp', 'cols'), may hold values from -0.09375 to 0.09375
- mix_share: float32 [4096], P('fsdp'), may hold values from 0.2 to 0.8
- norm_train: float32 [4096], P(('fsdp', 'cols')), may hold values from 0.25 to 1.75
- norm_step: float32 [4096], P(('fsdp', 'cols')), may hold values from -0.3 to 0.3
Outputs:
- final_query: bfloat16 [4096, 4096], P(None, 'cols')
- final_key: bfloat16 [4096, 4096], P(None, 'cols')
- final_value: bfloat16 [4096, 4096], P(None, 'cols')
- scale_query: float32 [4096], P('cols')
- scale_key: float32 [4096], P('cols')
- scale_value: float32 [4096], P('cols')
- serve_norm: bfloat16 [4096], replicated
All inputs are finite; a program needn't handle non-finite values.
Results may differ from a plain program's by a relative error of at most 0.0004.
Values may be sent and summed in bfloat16 or wider, within the bound.
A program may use at most 128 MiB of HBM per device.

v0:
```python
import jax
import jax.numpy as jnp
from jax import lax
from jax.sharding import PartitionSpec as P


def per_device(
    one_query,
    other_query,
    one_key,
    other_key,
    one_value,
    other_value,
    mix_share,
    norm_train,
    norm_step,
):
    result_query = mix_share[:, None] * one_query + (1.0 - mix_share[:, None]) * other_query
    result_key = mix_share[:, None] * one_key + (1.0 - mix_share[:, None]) * other_key
    result_value = mix_share[:, None] * one_value + (1.0 - mix_share[:, None]) * other_value
    total_query, total_key, total_value = lax.psum(
        (
            jnp.sum(result_query * result_query, axis=0),
            jnp.sum(result_key * result_key, axis=0),
            jnp.sum(result_value * result_value, axis=0),
        ),
        "fsdp",
    )
    scale_query = jnp.sqrt(total_query)
    scale_key = jnp.sqrt(total_key)
    scale_value = jnp.sqrt(total_value)
    narrow_query, narrow_key, narrow_value = (
        (result_query / scale_query).astype(jnp.bfloat16),
        (result_key / scale_key).astype(jnp.bfloat16),
        (result_value / scale_value).astype(jnp.bfloat16),
    )
    final_query, final_key, final_value = (
        lax.all_gather(narrow_query, "fsdp", axis=0, tiled=True),
        lax.all_gather(narrow_key, "fsdp", axis=0, tiled=True),
        lax.all_gather(narrow_value, "fsdp", axis=0, tiled=True),
    )
    serve_norm = lax.all_gather(
        (norm_train + norm_step).astype(jnp.bfloat16), ("fsdp", "cols"), axis=0, tiled=True
    )
    return (final_query, final_key, final_value, scale_query, scale_key, scale_value, serve_norm)


def solution(mesh):
    in_specs = (
        P("fsdp", "cols"),
        P("fsdp", "cols"),
        P("fsdp", "cols"),
        P("fsdp", "cols"),
        P("fsdp", "cols"),
        P("fsdp", "cols"),
        P("fsdp"),
        P(("fsdp", "cols")),
        P(("fsdp", "cols")),
    )
    out_specs = (
        P(None, "cols"),
        P(None, "cols"),
        P(None, "cols"),
        P("cols"),
        P("cols"),
        P("cols"),
        P(),
    )
    return jax.shard_map(
        per_device, mesh=mesh, in_specs=in_specs, out_specs=out_specs, check_vma=False
    )
```

profile of v0, /device:TPU:0, one launch (start us, length us, event | category | flops | bytes accessed | tf_op | source)
XLA Modules:
  0.0 326.6 jit_solution(14875302773791785755)
XLA Ops:
  7.2 0.0 all-gather.5.cloned.1.call-start
  7.2 0.7 broadcast_subtract_fusion
  7.9 0.0 copy-start
  7.9 0.0 copy-start.1
  7.9 6.6 %multiply_reduce_fusion = (f32[1024]{0:T(1024)S(1)}, f32[1024]{0:T(1024)S(1)}, f32[1024]{0:T(1024)S(1)}) fusion(f32[512,1024]{1,0:T(8,128)} %param.14, f32[512]{0:T(512)S(1)} %broadcast_subtract_fusion, f32[512,1024]{1,0:T(8,128)} %param.13, f32[512]{0:T(512)} %param.15, f32[512,1024]{1,0:T(8,128)} %param.12, f32[512,1024]{1,0:T(8,128)} %param.11, ...), kind=kLoop, calls=%fused_computation.1 | loop fusion | flops 7861248 | bytes 12599296 | tf_op jit(solution)/shard_map/reduce_sum | solution.py:25
  14.5 30.3 %all-reduce = (f32[1024]{0:T(1024)S(1)}, f32[1024]{0:T(1024)S(1)}, f32[1024]{0:T(1024)S(1)}) all-reduce(f32[1024]{0:T(1024)S(1)} %get-tuple-element.9, f32[1024]{0:T(1024)S(1)} %get-tuple-element.8, f32[1024]{0:T(1024)S(1)} %get-tuple-element.7), channel_id=1, replica_groups=mesh['fsdp'=8,'cols'=4] {'fsdp'}, use_global_device_ids=true, to_apply=%region_1.0 | all-reduce | flops 3072 | bytes 24576 | tf_op jit(solution)/shard_map/psum | solution.py:21
  44.8 0.0 copy-start.2
  44.8 0.0 copy-start.3
  44.8 0.0 copy-done
  44.8 0.0 copy-done.1
  44.8 0.0 copy-start.4
  44.8 6.1 %divide_convert_fusion = (bf16[512,1024]{1,0:T(8,128)(2,1)}, bf16[512,1024]{1,0:T(8,128)(2,1)}, bf16[512,1024]{1,0:T(8,128)(2,1)}) fusion(f32[1024]{0:T(1024)S(1)} %sqrt.11, f32[512,1024]{1,0:T(8,128)S(1)} %copy-done, f32[512]{0:T(512)S(1)} %broadcast_subtract_fusion, f32[512,1024]{1,0:T(8,128)} %param.13, f32[512]{0:T(512)S(1)} %copy-done.1, ...), kind=kLoop, calls=%fused_computation | loop fusion | flops 7864320 | bytes 15745024 | tf_op jit(solution)/shard_map/convert_element_type | solution.py:35
  50.9 0.0 copy-done.2
  50.9 0.0 copy-done.3
  50.9 0.0 copy-done.4
  50.9 0.0 copy-start.5
  50.9 0.0 copy-start.6
  50.9 0.0 all-gather.5.cloned.1.call-update
  51.0 0.0 all-gather.7.cloned.1.call-start
  51.0 0.7 all-gather.7.cloned.1.call-update
  51.7 0.0 all-gather.9.cloned.1.call-start
  51.8 0.7 all-gather.9.cloned.1.call-update
  52.5 0.0 copy-done.5
  52.5 0.0 copy-done.6
  52.5 67.5 %all-gather = bf16[32,1,128]{2,1,0:T(2,128)(2,1)S(1)} all-gather(bf16[1,1,128]{2,1,0:T(2,128)(2,1)S(1)} %convert_bitcast_fusion), channel_id=1, replica_groups=mesh['fsdp'=8,'cols'=4] {'fsdp','cols'}, dimensions={0}, use_global_device_ids=true | all-gather | bytes 8448 | tf_op jit(solution)/shard_map/all_gather | solution.py:42
  120.0 0.6 reduce
  120.6 10.7 %all-gather.5.cloned.1.call-done = bf16[4096,1024]{1,0:T(8,128)(2,1)} async-done(((bf16[512,1024]{1,0:T(8,128)(2,1)}), bf16[4096,1024]{1,0:T(8,128)(2,1)}) %all-gather.5.cloned.1.call-update) | async-done | bytes 8388624 | tf_op jit(solution)/shard_map/all_gather | solution.py:38
  131.4 82.7 %all-gather.7.cloned.1.call-done = bf16[4096,1024]{1,0:T(8,128)(2,1)} async-done(((bf16[512,1024]{1,0:T(8,128)(2,1)}), bf16[4096,1024]{1,0:T(8,128)(2,1)}) %all-gather.7.cloned.1.call-update) | async-done | bytes 8388624 | tf_op jit(solution)/shard_map/all_gather | solution.py:39
  214.1 82.7 %all-gather.9.cloned.1.call-done = bf16[4096,1024]{1,0:T(8,128)(2,1)} async-done(((bf16[512,1024]{1,0:T(8,128)(2,1)}), bf16[4096,1024]{1,0:T(8,128)(2,1)}) %all-gather.9.cloned.1.call-update) | async-done | bytes 8388624 | tf_op jit(solution)/shard_map/all_gather | solution.py:40
  296.8 7.8 %copy.19 = bf16[4096,1024]{1,0:T(8,128)(2,1)} copy(bf16[4096,1024]{1,0:T(8,128)(2,1)} %all-gather.5.cloned.1.call-done) | data formatting | bytes 16777216
  304.6 7.8 %copy.20 = bf16[4096,1024]{1,0:T(8,128)(2,1)} copy(bf16[4096,1024]{1,0:T(8,128)(2,1)} %all-gather.7.cloned.1.call-done) | data formatting | bytes 16777216
  312.3 7.8 %copy.21 = bf16[4096,1024]{1,0:T(8,128)(2,1)} copy(bf16[4096,1024]{1,0:T(8,128)(2,1)} %all-gather.9.cloned.1.call-done) | data formatting | bytes 16777216
  (4 shorter events, 0.0 us)
Async XLA Ops:
  7.2 124.2 %all-gather.5.cloned.1.call-start = ((), (), s32[]{:S(2)}) async-start(), calls=%async_computation | async-start | bytes 9437184 | tf_op jit(solution)/shard_map/all_gather | solution.py:38
  7.9 36.9 %copy-start = (f32[512,1024]{1,0:T(8,128)S(1)}, f32[512,1024]{1,0:T(8,128)}, u32[]{:S(2)}) copy-start(f32[512,1024]{1,0:T(8,128)} %param.14) | copy-start | bytes 6291460
  7.9 36.9 %copy-start.1 = (f32[512]{0:T(512)S(1)}, f32[512]{0:T(512)}, u32[]{:S(2)}) copy-start(f32[512]{0:T(512)} %param.15) | copy-start | bytes 6148
  44.8 6.1 %copy-start.2 = (f32[1024]{0:T(1024)}, f32[1024]{0:T(1024)S(1)}, u32[]{:S(2)}) copy-start(f32[1024]{0:T(1024)S(1)} %sqrt.10) | copy-start | bytes 12292
  44.8 6.1 %copy-start.3 = (f32[1024]{0:T(1024)}, f32[1024]{0:T(1024)S(1)}, u32[]{:S(2)}) copy-start(f32[1024]{0:T(1024)S(1)} %sqrt.11) | copy-start | bytes 12292
  44.8 6.1 %copy-start.4 = (f32[1024]{0:T(1024)}, f32[1024]{0:T(1024)S(1)}, u32[]{:S(2)}) copy-start(f32[1024]{0:T(1024)S(1)} %sqrt.9) | copy-start | bytes 12292
  50.9 1.5 copy-start.5
  50.9 1.5 copy-start.6
  51.0 163.1 %all-gather.7.cloned.1.call-start = ((), (), s32[]{:S(2)}) async-start(), calls=%async_computation.1 | async-start | bytes 9437184 | tf_op jit(solution)/shard_map/all_gather | solution.py:39
  51.7 245.1 %all-gather.9.cloned.1.call-start = ((), (), s32[]{:S(2)}) async-start(), calls=%async_computation.2 | async-start | bytes 9437184 | tf_op jit(solution)/shard_map/all_gather | solution.py:40
Sparse Core Ops, SparseCore 0:
  51.1 80.2 all-gather.4
  133.5 80.4 all-gather.6
  216.3 80.5 all-gather.8
where the time goes:
time: 327 us
  waiting for transfers between devices  178 us (54%)
  blocking collectives  97.8 us (30%)
  local copies, waits for them, and re-layouts  23.3 us (7%)
  other arithmetic  14 us (4%)
  between operations  13.8 us (4%)
    all_gather x1, waiting for transfers between devices, per_device(): lax.all_gather(narrow_value, 'fsdp', axis=0, tiled=True)  82.7 us
    all_gather x1, waiting for transfers between devices, per_device(): lax.all_gather(narrow_key, 'fsdp', axis=0, tiled=True)  82.7 us
    all_gather x1, blocking collectives, per_device(): lax.all_gather((norm_train + norm_step).astype(jnp.bfloat16), ('fsdp', 'c...  67.5 us
    psum x1, blocking collectives, per_device(): lax.psum((jnp.sum(result_query * result_query, axis=0), jnp.sum(result_ke...  30.3 us
    unnamed x17, local copies, waits for them, and re-layouts  23.3 us
    all_gather x1, waiting for transfers between devices, per_device(): lax.all_gather(narrow_query, 'fsdp', axis=0, tiled=True)  10.7 us
    reduce_sum x1, other arithmetic, per_device(): jnp.sum(result_value * result_value, axis=0)  6.57 us
  transfers between devices with their start and end apart: 3, of which 3 were waited for; matrix products, arithmetic and copies ran while one was open for 0% of the time, Pallas kernels for 0%

commit v1 on v0

v1 whole, which is shorter than its diff:
```python
import functools

import jax
import jax.numpy as jnp
from jax import lax
from jax.experimental import pallas as pl
from jax.experimental.pallas import tpu as pltpu
from jax.sharding import PartitionSpec as P

MESH = pl.DeviceIdType.MESH
LANES = 128
CHUNKS = 4


def gather_kernel(F, C, *refs):
    ins, mix_ref, train_ref, step_ref = refs[0:6], refs[6], refs[7], refs[8]
    outs, scale_out, norm_out = refs[9:12], refs[12], refs[13]
    (held, mixb, sums, in_sem, sum_send, sum_recv, norm_send1, norm_recv1,
     norm_send2, norm_recv2, up_send, down_send, pair_send, line_recv, pair_recv) = refs[14:]
    rows, width = ins[0].shape
    Z = F // 2
    me = lax.axis_index("fsdp")
    col = lax.axis_index("cols")
    z = me // 2
    core = lax.rem(me, 2)
    part = rows // CHUNKS
    K = 3 * CHUNKS

    def at(f):
        return {"fsdp": f}

    loads = [pltpu.make_async_copy(ins[i], held.at[i], in_sem.at[i]) for i in range(6)]
    for load in loads:
        load.start()

    barrier = pltpu.get_barrier_semaphore()
    for d in range(1, F):
        pl.semaphore_signal(barrier, inc=1, device_id=(lax.rem(me + d, F), col), device_id_type=MESH)
    for d in range(1, C):
        pl.semaphore_signal(barrier, inc=1, device_id=(me, lax.rem(col + d, C)), device_id_type=MESH)

    for g in range(rows // LANES):
        row = mix_ref[pl.ds(g, 1), :]
        mixb[pl.ds(g * LANES, LANES), :] = jnp.broadcast_to(row, (LANES, LANES)).T
    norm_out[me, col] = train_ref[...] + step_ref[...]

    def mix(a):
        loads[2 * a].wait()
        loads[2 * a + 1].wait()

        def body(i, acc):
            r = pl.ds(pl.multiple_of(i * 8, 8), 8)
            m = mixb[r, :]
            n = 1.0 - m
            new = []
            for j in range(width // LANES):
                c = pl.ds(j * LANES, LANES)
                v = m * held[2 * a, r, c] + n * held[2 * a + 1, r, c]
                held[2 * a, r, c] = v
                new.append(acc[j] + v * v)
            return tuple(new)

        zero = jnp.zeros((8, LANES), jnp.float32)
        acc = lax.fori_loop(0, rows // 8, body, (zero,) * (width // LANES), unroll=2)
        for j in range(width // LANES):
            sums[a, me, :, pl.ds(j * LANES, LANES)] = jnp.sum(acc[j], axis=0, keepdims=True)

    def sum_copy(a, d):
        peer = lax.rem(me + d, F)
        return pltpu.make_async_remote_copy(
            src_ref=sums.at[a, me], dst_ref=sums.at[a, me],
            send_sem=sum_send.at[a, d], recv_sem=sum_recv.at[a, me],
            device_id=(peer, col), device_id_type=MESH)

    def sum_arrival(a, f):
        return pltpu.make_async_remote_copy(
            src_ref=sums.at[a, f], dst_ref=sums.at[a, f],
            send_sem=sum_send.at[a, 0], recv_sem=sum_recv.at[a, f],
            device_id=(f, col), device_id_type=MESH)

    def norm_copy1(d):
        return pltpu.make_async_remote_copy(
            src_ref=norm_out.at[me, col], dst_ref=norm_out.at[me, col],
            send_sem=norm_send1.at[d], recv_sem=norm_recv1.at[col],
            device_id=(me, lax.rem(col + d, C)), device_id_type=MESH)

    def norm_copy2(d):
        return pltpu.make_async_remote_copy(
            src_ref=norm_out.at[me], dst_ref=norm_out.at[me],
            send_sem=norm_send2.at[d], recv_sem=norm_recv2.at[me],
            device_id=(lax.rem(me + d, F), col), device_id_type=MESH)

    mix(0)
    pl.semaphore_wait(barrier, F - 1 + C - 1)
    for d in range(1, F):
        sum_copy(0, d).start()
    for d in range(1, C):
        norm_copy1(d).start()
    mix(1)
    for d in range(1, F):
        sum_copy(1, d).start()
    mix(2)
    for d in range(1, F):
        sum_copy(2, d).start()

    def piece(a, source, q):
        start = pl.multiple_of(source * rows + q * part, part)
        return outs[a].at[pl.ds(start, part), :]

    def send(a, source, q, target, sender, receiver):
        ref = piece(a, source, q)
        return pltpu.make_async_remote_copy(
            src_ref=ref, dst_ref=ref, send_sem=sender, recv_sem=receiver,
            device_id=(target, col), device_id_type=MESH)

    def up(a, s, q):
        n = s * K + a * CHUNKS + q
        return send(a, 2 * s + core, q, me + 2, up_send.at[n], line_recv.at[n])

    def down(a, s, q):
        n = s * K + a * CHUNKS + q
        return send(a, 2 * s + core, q, me - 2, down_send.at[n], line_recv.at[n])

    def pair(a, s, q):
        n = s * K + a * CHUNKS + q
        return send(a, 2 * s + core, q, 2 * z + 1 - core, pair_send.at[n], pair_recv.at[n])

    def pair_arrival(a, s, q):
        n = s * K + a * CHUNKS + q
        return send(a, 2 * s + 1 - core, q, 2 * z + 1 - core, pair_send.at[n], pair_recv.at[n])

    def start_own(a, q):
        @pl.when(z > 0)
        def _():
            down(a, z, q).start()

        @pl.when(z < Z - 1)
        def _():
            up(a, z, q).start()

        pair(a, z, q).start()

    waiting = None
    for a in range(3):
        for d in range(1, F):
            sum_arrival(a, lax.rem(me + d, F)).wait_recv()
        total = sums[a, 0]
        for f in range(1, F):
            total = total + sums[a, f]
        scale = jnp.sqrt(total)
        scale_out[a] = scale
        inverse = jnp.broadcast_to(1.0 / scale, (16, width))
        for q in range(CHUNKS):
            base = me * rows + q * part

            def body(i, carry, a=a, q=q, base=base, inverse=inverse):
                r = pl.ds(pl.multiple_of(q * part + i * 16, 16), 16)
                o = pl.ds(pl.multiple_of(base + i * 16, 16), 16)
                outs[a][o, :] = (held[2 * a, r, :] * inverse).astype(jnp.bfloat16)
                return carry

            lax.fori_loop(0, part // 16, body, 0, unroll=2)
            if waiting is not None:
                start_own(*waiting)
            waiting = (a, q)
    for d in range(1, C):
        other = lax.rem(col + d, C)
        pltpu.make_async_remote_copy(
            src_ref=norm_out.at[me, other], dst_ref=norm_out.at[me, other],
            send_sem=norm_send1.at[0], recv_sem=norm_recv1.at[other],
            device_id=(me, other), device_id_type=MESH).wait_recv()
    for d in range(1, F):
        norm_copy2(d).start()
    start_own(*waiting)

    def relay(t, carry):
        hop = t // CHUNKS // 3 + 1
        q = lax.rem(t, CHUNKS)
        kind = lax.rem(t // CHUNKS, 3)
        for a in range(3):
            @pl.when(jnp.logical_and(kind == a, z + hop < Z))
            def _(a=a):
                down(a, z + hop, q).wait_recv()

                @pl.when(z > 0)
                def _():
                    down(a, z + hop, q).start()

                pair(a, z + hop, q).start()

            @pl.when(jnp.logical_and(kind == a, z - hop >= 0))
            def _(a=a):
                up(a, z - hop, q).wait_recv()

                @pl.when(z < Z - 1)
                def _():
                    up(a, z - hop, q).start()

                pair(a, z - hop, q).start()

        return carry

    lax.fori_loop(0, (Z - 1) * K, relay, 0)

    for d in range(1, F):
        f = lax.rem(me + d, F)
        pltpu.make_async_remote_copy(
            src_ref=norm_out.at[f], dst_ref=norm_out.at[f],
            send_sem=norm_send2.at[0], recv_sem=norm_recv2.at[f],
            device_id=(f, col), device_id_type=MESH).wait_recv()
        norm_copy2(d).wait_send()
        for a in range(3):
            sum_copy(a, d).wait_send()
    for d in range(1, C):
        norm_copy1(d).wait_send()

    def drain(n, carry):
        s = n // CHUNKS
        q = lax.rem(n, CHUNKS)
        for a in range(3):
            @pl.when(jnp.logical_and(z > 0, s >= z))
            def _(a=a):
                down(a, s, q).wait_send()

            @pl.when(jnp.logical_and(z < Z - 1, s <= z))
            def _(a=a):
                up(a, s, q).wait_send()

            pair_arrival(a, s, q).wait_recv()
            pair(a, s, q).wait_send()
        return carry

    lax.fori_loop(0, Z * CHUNKS, drain, 0)


def store_kernel(pieces, *refs):
    gathered, scales, norm = refs[0:3], refs[3], refs[4]
    finals, scale_outs, norm_out = refs[5:8], refs[8:11], refs[11]
    flat, sem = refs[12:]
    rows, width = gathered[0].shape
    part = rows // pieces
    copies = []
    for a in range(3):
        for p in range(pieces):
            r = pl.ds(p * part, part)
            copies.append(pltpu.make_async_copy(
                gathered[a].at[r, :], finals[a].at[r, :], sem.at[a * pieces + p]))
    for copy in copies:
        copy.start()
    for a in range(3):
        for j in range(width // LANES):
            scale_outs[a][pl.ds(j, 1), :] = scales[a, :, pl.ds(j * LANES, LANES)]
    F, C = norm.shape[0], norm.shape[1]
    for f in range(F):
        for c in range(C):
            flat[pl.ds(f * C + c, 1), :] = norm[f, c]
    norm_out[...] = flat[...].astype(jnp.bfloat16)
    for copy in copies:
        copy.wait()


def per_device(F, C, one_query, other_query, one_key, other_key, one_value, other_value,
               mix_share, norm_train, norm_step):
    rows, width = one_query.shape
    count = norm_train.shape[0]
    Z = F // 2
    K = 3 * CHUNKS
    whole = (F * rows, width)
    any_spec = pl.BlockSpec(memory_space=pl.ANY)
    vmem = pl.BlockSpec(memory_space=pltpu.VMEM)
    dma = pltpu.SemaphoreType.DMA
    sent = 3 * rows * width * 2 * Z
    gathered = pl.pallas_call(
        functools.partial(gather_kernel, F, C),
        out_shape=[pltpu.VMEM(whole, jnp.bfloat16)] * 3 + [
            pltpu.VMEM((3, 1, width), jnp.float32),
            pltpu.VMEM((F, C, 1, count), jnp.float32),
        ],
        in_specs=[pl.BlockSpec(memory_space=pltpu.HBM)] * 6 + [vmem] * 3,
        out_specs=[vmem] * 5,
        scratch_shapes=[
            pltpu.VMEM((6, rows, width), jnp.float32),
            pltpu.VMEM((rows, LANES), jnp.float32),
            pltpu.VMEM((3, F, 1, width), jnp.float32),
            dma((6,)),
            dma((3, F)), dma((3, F)),
            dma((C,)), dma((C,)),
            dma((F,)), dma((F,)),
            dma((Z * K,)), dma((Z * K,)), dma((Z * K,)), dma((Z * K,)), dma((Z * K,)),
        ],
        compiler_params=pltpu.CompilerParams(
            collective_id=0, has_side_effects=True, vmem_limit_bytes=VLIM),
        cost_estimate=pl.CostEstimate(flops=0, bytes_accessed=sent, transcendentals=0),
    )(one_query, other_query, one_key, other_key, one_value, other_value,
      mix_share.reshape(rows // LANES, LANES), norm_train.reshape(1, count),
      norm_step.reshape(1, count))
    pieces = 4
    finals = pl.pallas_call(
        functools.partial(store_kernel, pieces),
        out_shape=[jax.ShapeDtypeStruct(whole, jnp.bfloat16)] * 3
        + [jax.ShapeDtypeStruct((width // LANES, LANES), jnp.float32)] * 3
        + [jax.ShapeDtypeStruct((F * C, count), jnp.bfloat16)],
        in_specs=[vmem] * 5,
        out_specs=[any_spec] * 3 + [vmem] * 4,
        scratch_shapes=[pltpu.VMEM((F * C, count), jnp.float32), dma((3 * pieces,))],
        compiler_params=pltpu.CompilerParams(vmem_limit_bytes=VLIM2),
    )(*gathered)
    return (*finals[:3], *(s.reshape(width) for s in finals[3:6]), finals[6].reshape(F * C * count))


VLIM = 36 * 1024 * 1024
VLIM2 = 2 * 1024 * 1024


def solution(mesh):
    F, C = mesh.shape["fsdp"], mesh.shape["cols"]
    block, fsdp, both = P("fsdp", "cols"), P("fsdp"), P(("fsdp", "cols"))
    return jax.shard_map(
        functools.partial(per_device, F, C), mesh=mesh,
        in_specs=(block,) * 6 + (fsdp, both, both),
        out_specs=(P(None, "cols"),) * 3 + (P("cols"),) * 3 + (P(),),
        check_vma=False)
```

time: 327 us -> 228 us (0.70)
  Pallas kernels: 0 us -> 228 us
  waiting for transfers between devices: 178 us -> 0 us
  blocking collectives: 97.8 us -> 0 us
  local copies, waits for them, and re-layouts: 23.3 us -> 0 us
  other arithmetic: 14 us -> 0 us
  between operations: 13.8 us -> 0.64 us
    pallas_call x0 -> x2, Pallas kernels: none -> 228 us  [the longest x1 219 us: per_device(): pl.pallas_call(functools.partial(gather_kernel, F, C), out_shape=[pltpu.V...]
    all_gather x3 -> x0, waiting for transfers between devices: 176 us -> none  [the longest x1 82.7 us: per_device(): lax.all_gather(narrow_value, 'fsdp', axis=0, tiled=True)]
    all_gather x1 -> x0, blocking collectives: 67.5 us -> none  [per_device(): lax.all_gather((norm_train + norm_step).astype(jnp.bfloat16), ('fsdp', 'c...]
    psum x1 -> x0, blocking collectives: 30.3 us -> none  [per_device(): lax.psum((jnp.sum(result_query * result_query, axis=0), jnp.sum(result_ke...]
    unnamed x17 -> x0, local copies, waits for them, and re-layouts: 23.3 us -> none
    reduce_sum x1 -> x0, other arithmetic: 6.57 us -> none  [per_device(): jnp.sum(result_value * result_value, axis=0)]
    convert_element_type x1 -> x0, other arithmetic: 6.06 us -> none  [per_device(): (result_value / scale_value).astype(jnp.bfloat16)]
  transfers between devices with their start and end apart: 3 -> 0, of which waited for: 3 -> 0; matrix products, arithmetic and copies ran while one was open for 0% -> 0% of each run, Pallas kernels for 0% -> 0%
where the time goes in v1:
time: 228 us
  Pallas kernels  228 us (100%)
    pallas_call x1, Pallas kernels, per_device(): pl.pallas_call(functools.partial(gather_kernel, F, C), out_shape=[pltpu.V...  219 us
    pallas_call x1, Pallas kernels, per_device(): pl.pallas_call(functools.partial(store_kernel, pieces), out_shape=[jax.Sh...  9.09 us

profile of v1, /device:TPU:0, one launch (start us, length us, event | category | flops | bytes accessed | tf_op | source)
XLA Modules:
  0.0 228.3 jit_solution(10276293740993266272)
XLA Ops:
  0.6 218.6 %shard_map.144 = (bf16[4096,1024]{1,0:T(8,128)(2,1)S(1)}, bf16[4096,1024]{1,0:T(8,128)(2,1)S(1)}, bf16[4096,1024]{1,0:T(8,128)(2,1)S(1)}, f32[3,1,1024]{2,1,0:T(1,128)S(1)}, f32[8,4,1,128]{3,2,1,0:T(1,128)S(1)}) custom-call(f32[512,1024]{1,0:T(8,128)} %refs_0_.1, f32[512,1024]{1,0:T(8,128)} %refs_1_.1, f32[512,1024]{1,0:T(8,128)} %refs_2_.1, ...), custom_call_target="tpu_custom_call" | custom-call | bytes 12582912 | tf_op jit(solution)/shard_map/pallas_call | solution.py:273
  219.2 9.1 %shard_map.145 = (bf16[4096,1024]{1,0:T(8,128)(2,1)}, bf16[4096,1024]{1,0:T(8,128)(2,1)}, bf16[4096,1024]{1,0:T(8,128)(2,1)}, f32[8,128]{1,0:T(8,128)}, f32[8,12...) custom-call(bf16[4096,1024]{1,0:T(8,128)(2,1)S(1)} %get-tuple-element.19.refs_0_, ...), custom_call_target="tpu_custom_call" | custom-call | tf_op jit(solution)/shard_map/pallas_call | solution.py:298

commit v2 on v1

v2 whole, which is shorter than its diff:
```python
import functools

import jax
import jax.numpy as jnp
from jax import lax
from jax.experimental import pallas as pl
from jax.experimental.pallas import tpu as pltpu
from jax.sharding import PartitionSpec as P

MESH = pl.DeviceIdType.MESH
LANES = 128
PIECES = ((0, 0, 1), (0, 1, 1), (0, 2, 6), (1, 0, 8), (2, 0, 6), (2, 6, 2))
LOADS = 4


def gather_kernel(F, C, *refs):
    ins, mix_ref, train_ref, step_ref = refs[0:6], refs[6], refs[7], refs[8]
    outs, scale_out, norm_out = refs[9:12], refs[12], refs[13]
    (held, mixb, sums, in_sem, sum_send, sum_recv, norm_send1, norm_recv1,
     norm_send2, norm_recv2, up_send, down_send, pair_send, line_recv, pair_recv,
     early, early_send, early_recv) = refs[14:]
    rows, width = ins[0].shape
    Z = F // 2
    me = lax.axis_index("fsdp")
    col = lax.axis_index("cols")
    z = me // 2
    core = lax.rem(me, 2)
    eighth = rows // 8
    K = len(PIECES)

    def at(f):
        return {"fsdp": f}

    load_rows = rows // LOADS

    def load(i, p):
        r = pl.ds(p * load_rows, load_rows)
        return pltpu.make_async_copy(ins[i].at[r, :], held.at[i, r, :], in_sem.at[i, p])

    for p in range(LOADS):
        load(0, p).start()
        load(1, p).start()

    barrier = pltpu.get_barrier_semaphore()
    for d in range(1, F):
        pl.semaphore_signal(barrier, inc=1, device_id=(lax.rem(me + d, F), col), device_id_type=MESH)
    for d in range(1, C):
        pl.semaphore_signal(barrier, inc=1, device_id=(me, lax.rem(col + d, C)), device_id_type=MESH)

    for g in range(rows // LANES):
        row = mix_ref[pl.ds(g, 1), :]
        mixb[pl.ds(g * LANES, LANES), :] = jnp.broadcast_to(row, (LANES, LANES)).T
    norm_out[me, col] = train_ref[...] + step_ref[...]

    def mix(a):
        def body(i, acc):
            r = pl.ds(pl.multiple_of(i * 8, 8), 8)
            m = mixb[r, :]
            n = 1.0 - m
            new = []
            for j in range(width // LANES):
                c = pl.ds(j * LANES, LANES)
                v = m * held[2 * a, r, c] + n * held[2 * a + 1, r, c]
                held[2 * a, r, c] = v
                new.append(acc[j] + v * v)
            return tuple(new)

        zero = jnp.zeros((8, LANES), jnp.float32)
        acc = (zero,) * (width // LANES)
        for p in range(LOADS):
            load(2 * a, p).wait()
            load(2 * a + 1, p).wait()
            acc = lax.fori_loop(p * load_rows // 8, (p + 1) * load_rows // 8, body, acc, unroll=2)
            if a == 0 and p == LOADS - 2:
                for i in range(2, 6):
                    for later in range(LOADS):
                        load(i, later).start()
        for j in range(width // LANES):
            sums[a, me, :, pl.ds(j * LANES, LANES)] = jnp.sum(acc[j], axis=0, keepdims=True)

    def sum_copy(a, d):
        peer = lax.rem(me + d, F)
        return pltpu.make_async_remote_copy(
            src_ref=sums.at[a, me], dst_ref=sums.at[a, me],
            send_sem=sum_send.at[a, d], recv_sem=sum_recv.at[a, me],
            device_id=(peer, col), device_id_type=MESH)

    def sum_arrival(a, f):
        return pltpu.make_async_remote_copy(
            src_ref=sums.at[a, f], dst_ref=sums.at[a, f],
            send_sem=sum_send.at[a, 0], recv_sem=sum_recv.at[a, f],
            device_id=(f, col), device_id_type=MESH)

    def norm_copy1(d):
        return pltpu.make_async_remote_copy(
            src_ref=norm_out.at[me, col], dst_ref=norm_out.at[me, col],
            send_sem=norm_send1.at[d], recv_sem=norm_recv1.at[col],
            device_id=(me, lax.rem(col + d, C)), device_id_type=MESH)

    def norm_copy2(d):
        return pltpu.make_async_remote_copy(
            src_ref=norm_out.at[me], dst_ref=norm_out.at[me],
            send_sem=norm_send2.at[d], recv_sem=norm_recv2.at[me],
            device_id=(lax.rem(me + d, F), col), device_id_type=MESH)

    mix(0)
    pl.semaphore_wait(barrier, F - 1 + C - 1)
    for d in range(1, F):
        sum_copy(0, d).start()
    early_rows = pl.ds(0, eighth)
    early_down = pltpu.make_async_remote_copy(
        src_ref=held.at[0, early_rows, :], dst_ref=early, send_sem=early_send.at[0],
        recv_sem=early_recv, device_id=(me - 2, col), device_id_type=MESH)
    early_up = pltpu.make_async_remote_copy(
        src_ref=held.at[0, early_rows, :], dst_ref=early, send_sem=early_send.at[1],
        recv_sem=early_recv, device_id=(me + 2, col), device_id_type=MESH)

    @pl.when(z == 1)
    def _():
        early_down.start()

    @pl.when(z == Z - 2)
    def _():
        early_up.start()

    for d in range(1, C):
        norm_copy1(d).start()
    mix(1)
    for d in range(1, F):
        sum_copy(1, d).start()
    mix(2)
    for d in range(1, F):
        sum_copy(2, d).start()

    def send(k, source, target, sender, receiver):
        a, first, count = PIECES[k]
        start = pl.multiple_of(source * rows + first * eighth, eighth)
        ref = outs[a].at[pl.ds(start, count * eighth), :]
        return pltpu.make_async_remote_copy(
            src_ref=ref, dst_ref=ref, send_sem=sender, recv_sem=receiver,
            device_id=(target, col), device_id_type=MESH)

    def up(k, s):
        n = s * K + k
        return send(k, 2 * s + core, me + 2, up_send.at[n], line_recv.at[n])

    def down(k, s):
        n = s * K + k
        return send(k, 2 * s + core, me - 2, down_send.at[n], line_recv.at[n])

    def pair(k, s):
        n = s * K + k
        return send(k, 2 * s + core, 2 * z + 1 - core, pair_send.at[n], pair_recv.at[n])

    def pair_arrival(k, s):
        n = s * K + k
        return send(k, 2 * s + 1 - core, 2 * z + 1 - core, pair_send.at[n], pair_recv.at[n])

    def goes_down(k, s):
        return jnp.logical_and(z > 0, jnp.logical_or(z != 1, s != z)) if k == 0 else z > 0

    def goes_up(k, s):
        return jnp.logical_and(z < Z - 1, jnp.logical_or(z != Z - 2, s != z)) if k == 0 else z < Z - 1

    def start_own(k):
        @pl.when(goes_down(k, z))
        def _():
            down(k, z).start()

        @pl.when(goes_up(k, z))
        def _():
            up(k, z).start()

        pair(k, z).start()

    def normalize(a, source, target, count, inverse):
        def body(i, carry):
            r = pl.ds(pl.multiple_of(i * 16, 16), 16)
            o = pl.ds(pl.multiple_of(target + i * 16, 16), 16)
            outs[a][o, :] = (source[r, :] * inverse).astype(jnp.bfloat16)
            return carry

        lax.fori_loop(0, count // 16, body, 0, unroll=2)

    inverses = []
    for k, (a, first, count) in enumerate(PIECES):
        if len(inverses) == a:
            for d in range(1, F):
                sum_arrival(a, lax.rem(me + d, F)).wait_recv()
            total = sums[a, 0]
            for f in range(1, F):
                total = total + sums[a, f]
            scale = jnp.sqrt(total)
            scale_out[a] = scale
            inverses.append(1.0 / scale)
        inverse = jnp.broadcast_to(inverses[a], (16, width))
        size = count * eighth
        normalize(a, held.at[2 * a, pl.ds(first * eighth, size), :],
                  me * rows + first * eighth, size, inverse)
        if k > 0:
            start_own(k - 1)
    for d in range(1, C):
        other = lax.rem(col + d, C)
        pltpu.make_async_remote_copy(
            src_ref=norm_out.at[me, other], dst_ref=norm_out.at[me, other],
            send_sem=norm_send1.at[0], recv_sem=norm_recv1.at[other],
            device_id=(me, other), device_id_type=MESH).wait_recv()
    for d in range(1, F):
        norm_copy2(d).start()
    start_own(K - 1)

    def take_early(owner):
        early_down.wait_recv()
        inverse = jnp.broadcast_to(1.0 / scale_out[0], (16, width))
        normalize(0, early, (2 * owner + core) * rows, eighth, inverse)

    def relay(hop, carry):
        for k in range(K):
            @pl.when(z + hop < Z)
            def _(k=k):
                if k == 0:
                    is_early = jnp.logical_and(z == 0, hop == 1)

                    @pl.when(is_early)
                    def _():
                        take_early(1)

                    @pl.when(jnp.logical_not(is_early))
                    def _():
                        down(k, z + hop).wait_recv()
                else:
                    down(k, z + hop).wait_recv()

                @pl.when(z > 0)
                def _():
                    down(k, z + hop).start()

                pair(k, z + hop).start()

            @pl.when(z - hop >= 0)
            def _(k=k):
                if k == 0:
                    is_early = jnp.logical_and(z == Z - 1, hop == 1)

                    @pl.when(is_early)
                    def _():
                        take_early(Z - 2)

                    @pl.when(jnp.logical_not(is_early))
                    def _():
                        up(k, z - hop).wait_recv()
                else:
                    up(k, z - hop).wait_recv()

                @pl.when(z < Z - 1)
                def _():
                    up(k, z - hop).start()

                pair(k, z - hop).start()

        return carry

    lax.fori_loop(1, Z, relay, 0)

    @pl.when(z == 1)
    def _():
        early_down.wait_send()

    @pl.when(z == Z - 2)
    def _():
        early_up.wait_send()

    for d in range(1, F):
        f = lax.rem(me + d, F)
        pltpu.make_async_remote_copy(
            src_ref=norm_out.at[f], dst_ref=norm_out.at[f],
            send_sem=norm_send2.at[0], recv_sem=norm_recv2.at[f],
            device_id=(f, col), device_id_type=MESH).wait_recv()
        norm_copy2(d).wait_send()
        for a in range(3):
            sum_copy(a, d).wait_send()
    for d in range(1, C):
        norm_copy1(d).wait_send()

    def drain(s, carry):
        for k in range(K):
            @pl.when(jnp.logical_and(goes_down(k, s), s >= z))
            def _(k=k):
                down(k, s).wait_send()

            @pl.when(jnp.logical_and(goes_up(k, s), s <= z))
            def _(k=k):
                up(k, s).wait_send()

            pair_arrival(k, s).wait_recv()
            pair(k, s).wait_send()
        return carry

    lax.fori_loop(0, Z, drain, 0)


def store_kernel(pieces, *refs):
    gathered, scales, norm = refs[0:3], refs[3], refs[4]
    finals, scale_outs, norm_out = refs[5:8], refs[8:11], refs[11]
    flat, flat_norm, flat_scales, sem, small_sem = refs[12:]
    rows, width = gathered[0].shape
    part = rows // pieces
    copies = []
    for a in range(3):
        for p in range(pieces):
            r = pl.ds(p * part, part)
            copies.append(pltpu.make_async_copy(
                gathered[a].at[r, :], finals[a].at[r, :], sem.at[a * pieces + p]))
    for copy in copies:
        copy.start()
    for a in range(3):
        for j in range(width // LANES):
            flat_scales[a, pl.ds(j, 1), :] = scales[a, :, pl.ds(j * LANES, LANES)]
    F, C = norm.shape[0], norm.shape[1]
    for f in range(F):
        for c in range(C):
            flat[pl.ds(f * C + c, 1), :] = norm[f, c]
    flat_norm[...] = flat[...].astype(jnp.bfloat16)
    small = [pltpu.make_async_copy(flat_scales.at[a], scale_outs[a], small_sem.at[a]) for a in range(3)]
    small.append(pltpu.make_async_copy(flat_norm, norm_out, small_sem.at[3]))
    for copy in small:
        copy.start()
    copies += small
    for copy in copies:
        copy.wait()


def per_device(F, C, one_query, other_query, one_key, other_key, one_value, other_value,
               mix_share, norm_train, norm_step):
    rows, width = one_query.shape
    count = norm_train.shape[0]
    Z = F // 2
    K = len(PIECES)
    whole = (F * rows, width)
    any_spec = pl.BlockSpec(memory_space=pl.ANY)
    vmem = pl.BlockSpec(memory_space=pltpu.VMEM)
    dma = pltpu.SemaphoreType.DMA
    sent = 3 * rows * width * 2 * Z
    gathered = pl.pallas_call(
        functools.partial(gather_kernel, F, C),
        out_shape=[pltpu.VMEM(whole, jnp.bfloat16)] * 3 + [
            pltpu.VMEM((3, 1, width), jnp.float32),
            pltpu.VMEM((F, C, 1, count), jnp.float32),
        ],
        in_specs=[pl.BlockSpec(memory_space=pltpu.HBM)] * 6 + [vmem] * 3,
        out_specs=[vmem] * 5,
        scratch_shapes=[
            pltpu.VMEM((6, rows, width), jnp.float32),
            pltpu.VMEM((rows, LANES), jnp.float32),
            pltpu.VMEM((3, F, 1, width), jnp.float32),
            dma((6, LOADS)),
            dma((3, F)), dma((3, F)),
            dma((C,)), dma((C,)),
            dma((F,)), dma((F,)),
            dma((Z * K,)), dma((Z * K,)), dma((Z * K,)), dma((Z * K,)), dma((Z * K,)),
            pltpu.VMEM((rows // 8, width), jnp.float32), dma((2,)), dma,
        ],
        compiler_params=pltpu.CompilerParams(
            collective_id=0, has_side_effects=True, vmem_limit_bytes=VLIM),
        cost_estimate=pl.CostEstimate(flops=0, bytes_accessed=sent, transcendentals=0),
    )(one_query, other_query, one_key, other_key, one_value, other_value,
      mix_share.reshape(rows // LANES, LANES), norm_train.reshape(1, count),
      norm_step.reshape(1, count))
    pieces = 4
    finals = pl.pallas_call(
        functools.partial(store_kernel, pieces),
        out_shape=[jax.ShapeDtypeStruct(whole, jnp.bfloat16)] * 3
        + [jax.ShapeDtypeStruct((width // LANES, LANES), jnp.float32)] * 3
        + [jax.ShapeDtypeStruct((F * C, count), jnp.bfloat16)],
        in_specs=[vmem] * 5,
        out_specs=[any_spec] * 7,
        scratch_shapes=[
            pltpu.VMEM((F * C, count), jnp.float32), pltpu.VMEM((F * C, count), jnp.bfloat16),
            pltpu.VMEM((3, width // LANES, LANES), jnp.float32), dma((3 * pieces,)), dma((4,)),
        ],
        compiler_params=pltpu.CompilerParams(vmem_limit_bytes=VLIM2),
    )(*gathered)
    return (*finals[:3], *(s.reshape(width) for s in finals[3:6]), finals[6].reshape(F * C * count))


VLIM = 36 * 1024 * 1024
VLIM2 = 2 * 1024 * 1024


def solution(mesh):
    F, C = mesh.shape["fsdp"], mesh.shape["cols"]
    block, fsdp, both = P("fsdp", "cols"), P("fsdp"), P(("fsdp", "cols"))
    return jax.shard_map(
        functools.partial(per_device, F, C), mesh=mesh,
        in_specs=(block,) * 6 + (fsdp, both, both),
        out_specs=(P(None, "cols"),) * 3 + (P("cols"),) * 3 + (P(),),
        check_vma=False)
```

time: 228 us -> 227 us (level)
  no operation moved by 1% of the time
where the time goes in v2:
time: 227 us
  Pallas kernels  226 us (100%)
    pallas_call x1, Pallas kernels, per_device(): pl.pallas_call(functools.partial(gather_kernel, F, C), out_shape=[pltpu.V...  217 us
    pallas_call x1, Pallas kernels, per_device(): pl.pallas_call(functools.partial(store_kernel, pieces), out_shape=[jax.Sh...  8.54 us

profile of v2, /device:TPU:0, one launch (start us, length us, event | category | flops | bytes accessed | tf_op | source)
XLA Modules:
  0.0 226.5 jit_solution(17225753619265927342)
XLA Ops:
  0.6 217.3 %shard_map.144 = (bf16[4096,1024]{1,0:T(8,128)(2,1)S(1)}, bf16[4096,1024]{1,0:T(8,128)(2,1)S(1)}, bf16[4096,1024]{1,0:T(8,128)(2,1)S(1)}, f32[3,1,1024]{2,1,0:T(1,128)S(1)}, f32[8,4,1,128]{3,2,1,0:T(1,128)S(1)}) custom-call(f32[512,1024]{1,0:T(8,128)} %refs_0_.1, f32[512,1024]{1,0:T(8,128)} %refs_1_.1, f32[512,1024]{1,0:T(8,128)} %refs_2_.1, ...), custom_call_target="tpu_custom_call" | custom-call | bytes 12582912 | tf_op jit(solution)/shard_map/pallas_call | solution.py:344
  218.0 8.5 %shard_map.145 = (bf16[4096,1024]{1,0:T(8,128)(2,1)}, bf16[4096,1024]{1,0:T(8,128)(2,1)}, bf16[4096,1024]{1,0:T(8,128)(2,1)}, f32[8,128]{1,0:T(8,128)}, f32[8,12...) custom-call(bf16[4096,1024]{1,0:T(8,128)(2,1)S(1)} %get-tuple-element.19.refs_0_, ...), custom_call_target="tpu_custom_call" | custom-call | tf_op jit(solution)/shard_map/pallas_call | solution.py:370
